TPU v7x, 32 devices: a whole 2x2x4 slice. The times are simulated.
32 devices in a mesh: wide: 8 (over y, x, core), head: 4 (over z).
Axes of the slice: x: 2, y: 2, z: 4, core: 2. Of those that a mesh axis runs over, the one named last changes fastest.
Arguments:
- tokens: bfloat16 [16384, 1024], P(('wide', 'head')), may hold values from -6 to 6
- cotangent: bfloat16 [16384, 1024], P(('wide', 'head')), may hold values from -6 to 6
- w_query: bfloat16 [1024, 1024], P('wide', 'head'), may hold values from -0.25 to 0.25
- w_key: bfloat16 [1024, 1024], P('wide', 'head'), may hold values from -0.25 to 0.25
- w_value: bfloat16 [1024, 1024], P('wide', 'head'), may hold values from -0.1875 to 0.1875
- w_out: bfloat16 [1024, 1024], P('head', 'wide'), may hold values from -0.1875 to 0.1875
- w_up: bfloat16 [1024, 4096], P('wide', 'head'), may hold values from -0.1875 to 0.1875
- w_down: bfloat16 [4096, 1024], P('head', 'wide'), may hold values from -0.09375 to 0.09375
- norm_gain: float32 [4, 1024], replicated, may hold values from 0.25 to 1.75
- norm_bias: float32 [4, 1024], replicated, may hold values from -3 to 3
Outputs:
- block_out: bfloat16 [16384, 1024], P(('wide', 'head'))
- input_grad: float32 [16384, 1024], P(('wide', 'head'))
- grad_query: float32 [1024, 1024], P('wide', 'head')
- grad_key: float32 [1024, 1024], P('wide', 'head')
- grad_value: float32 [1024, 1024], P('wide', 'head')
- grad_out: float32 [1024, 1024], P('head', 'wide')
- grad_up: float32 [1024, 4096], P('wide', 'head')
- grad_down: float32 [4096, 1024], P('head', 'wide')
- gain_grad: float32 [4, 1024], replicated
- bias_grad: float32 [4, 1024], replicated
All inputs are finite; a program needn't handle non-finite values.
Results may differ from a plain program's by a relative error of at most 0.015.
Values may be sent and summed in bfloat16 or wider, within the bound.
No kernel may reach another device: no remote copies, remote signals or barrier semaphores. Data moves between devices by JAX's collectives and lax.ppermute only.
A program may use at most 192 MiB of HBM per device.

v0:
```python
import math
import jax
import jax.numpy as jnp
from jax import lax
from jax.sharding import PartitionSpec as P

HD = 64
EPS = 1e-05


def normalize(values, gain, bias):
    average = jnp.mean(values, axis=-1, keepdims=True)
    centred = values - average
    inverse = lax.rsqrt(jnp.mean(centred * centred, axis=-1, keepdims=True) + EPS)
    unit_rows = centred * inverse
    return (unit_rows * gain + bias, unit_rows, inverse)


def normalize_back(gradient, unit_rows, inverse, gain):
    scaled = gradient * gain
    inner_sum = (
        scaled
        - jnp.mean(scaled, axis=-1, keepdims=True)
        - unit_rows * jnp.mean(scaled * unit_rows, axis=-1, keepdims=True)
    )
    return (inner_sum * inverse, jnp.sum(gradient * unit_rows, axis=0), jnp.sum(gradient, axis=0))


def rows_in(values):
    return lax.all_gather(values, "head", axis=0, tiled=True)


def grads_in(values):
    return lax.all_gather(values, "head", axis=0, tiled=True)


def branch_sum(left_op, right_op):
    return lax.psum_scatter(
        jnp.dot(left_op, right_op, preferred_element_type=jnp.float32),
        "head",
        scatter_dimension=0,
        tiled=True,
    )


def input_sum(operand_pairs):
    summed = None
    for left_op, right_op in operand_pairs:
        partial_value = lax.dot_general(
            left_op, right_op, (((1,), (1,)), ((), ())), preferred_element_type=jnp.float32
        )
        summed = partial_value if summed is None else summed + partial_value
    return lax.psum_scatter(summed, "head", scatter_dimension=0, tiled=True)


def masked_scores(rows_q, key_heads, first_row, score_scale):
    scores = (
        jnp.einsum("qgd,kgd->gqk", rows_q, key_heads, preferred_element_type=jnp.float32)
        * score_scale
    )
    place_q = first_row + jnp.arange(rows_q.shape[0], dtype=jnp.int32)
    place_k = jnp.arange(key_heads.shape[0], dtype=jnp.int32)
    allowed = place_k[None, :] <= place_q[:, None]
    return jnp.where(allowed[None], scores, -1e30)


def attend(queries, key_rows, value_rows, block_rows):
    length, width = queries.shape
    groups = width // HD
    score_scale = 1.0 / math.sqrt(HD)
    query_heads = queries.reshape(length, groups, HD)
    key_heads = key_rows.reshape(length, groups, HD)
    value_heads = value_rows.reshape(length, groups, HD)
    out_blocks = []
    totals = []
    for position in range(length // block_rows):
        first_row = position * block_rows
        last_row = first_row + block_rows
        scores = masked_scores(
            query_heads[first_row:last_row], key_heads[:last_row], first_row, score_scale
        )
        row_max = jnp.max(scores, axis=-1, keepdims=True)
        exp_scores = jnp.exp(scores - row_max)
        row_total = jnp.sum(exp_scores, axis=-1, keepdims=True)
        weights = (exp_scores / row_total).astype(jnp.bfloat16)
        out_blocks.append(
            jnp.einsum(
                "gqk,kgd->qgd", weights, value_heads[:last_row], preferred_element_type=jnp.float32
            )
        )
        totals.append(row_max + jnp.log(row_total))
    return (jnp.concatenate(out_blocks, axis=0).reshape(length, width), totals)


def attend_back(queries, key_rows, value_rows, grad_rows, totals, block_rows):
    length, width = queries.shape
    groups = width // HD
    score_scale = 1.0 / math.sqrt(HD)
    query_heads = queries.reshape(length, groups, HD)
    key_heads = key_rows.reshape(length, groups, HD)
    value_heads = value_rows.reshape(length, groups, HD)
    grad_heads = grad_rows.reshape(length, groups, HD)
    grad_keys = jnp.zeros((length, groups, HD), jnp.float32)
    grad_values = jnp.zeros((length, groups, HD), jnp.float32)
    query_parts = []
    for position in range(length // block_rows):
        first_row = position * block_rows
        last_row = first_row + block_rows
        rows_q = query_heads[first_row:last_row]
        scores = masked_scores(rows_q, key_heads[:last_row], first_row, score_scale)
        weights = jnp.exp(scores - totals[position])
        rounded = weights.astype(jnp.bfloat16)
        grad_block = grad_heads[first_row:last_row]
        grad_values = grad_values.at[:last_row].add(
            jnp.einsum("gqk,qgd->kgd", rounded, grad_block, preferred_element_type=jnp.float32)
        )
        grad_weights = jnp.einsum(
            "qgd,kgd->gqk", grad_block, value_heads[:last_row], preferred_element_type=jnp.float32
        )
        inner_sum = jnp.sum(weights * grad_weights, axis=-1, keepdims=True)
        grad_scores = (weights * (grad_weights - inner_sum)).astype(jnp.bfloat16)
        query_parts.append(
            jnp.einsum(
                "gqk,kgd->qgd",
                grad_scores,
                key_heads[:last_row],
                preferred_element_type=jnp.float32,
            )
            * score_scale
        )
        grad_keys = grad_keys.at[:last_row].add(
            jnp.einsum("gqk,qgd->kgd", grad_scores, rows_q, preferred_element_type=jnp.float32)
            * score_scale
        )
    grad_queries = jnp.concatenate(query_parts, axis=0).reshape(length, width).astype(jnp.bfloat16)
    return (
        grad_queries,
        grad_keys.reshape(length, width).astype(jnp.bfloat16),
        grad_values.reshape(length, width).astype(jnp.bfloat16),
    )


def contract_rows(left_op, right_op):
    return lax.dot_general(
        left_op, right_op, (((0,), (0,)), ((), ())), preferred_element_type=jnp.float32
    )


def contract_cols(left_op, right_op):
    return lax.dot_general(
        left_op, right_op, (((1,), (1,)), ((), ())), preferred_element_type=jnp.float32
    )


def on_device(
    tokens, cotangent, w_query, w_key, w_value, w_out, w_up, w_down, norm_gain, norm_bias
):
    full_q, full_k, full_v, full_o, full_up, full_down = (
        lax.all_gather(w_query, "wide", axis=0, tiled=True),
        lax.all_gather(w_key, "wide", axis=0, tiled=True),
        lax.all_gather(w_value, "wide", axis=0, tiled=True),
        lax.all_gather(w_out, "wide", axis=1, tiled=True),
        lax.all_gather(w_up, "wide", axis=0, tiled=True),
        lax.all_gather(w_down, "wide", axis=1, tiled=True),
    )
    residual = tokens.astype(jnp.float32)
    norm_a, unit_a, inv_a = normalize(residual, norm_gain[0], norm_bias[0])
    seq_a = rows_in(norm_a.astype(jnp.bfloat16))
    block_rows = min(512, seq_a.shape[0])
    queries = jnp.dot(seq_a, full_q, preferred_element_type=jnp.float32).astype(jnp.bfloat16)
    key_rows = jnp.dot(seq_a, full_k, preferred_element_type=jnp.float32).astype(jnp.bfloat16)
    value_rows = jnp.dot(seq_a, full_v, preferred_element_type=jnp.float32).astype(jnp.bfloat16)
    attended, totals = attend(queries, key_rows, value_rows, block_rows)
    attended = attended.astype(jnp.bfloat16)
    mixed = branch_sum(attended, full_o)
    norm_z, unit_z, inv_z = normalize(mixed, norm_gain[1], norm_bias[1])
    hidden = residual + norm_z
    norm_c, unit_c, inv_c = normalize(hidden, norm_gain[2], norm_bias[2])
    seq_c = rows_in(norm_c.astype(jnp.bfloat16))
    pre_act = jnp.dot(seq_c, full_up, preferred_element_type=jnp.float32)
    active, gelu_back = jax.vjp(jax.nn.gelu, pre_act)
    active = active.astype(jnp.bfloat16)
    output = branch_sum(active, full_down)
    norm_m, unit_m, inv_m = normalize(output, norm_gain[3], norm_bias[3])
    block_out = (hidden + norm_m).astype(jnp.bfloat16)
    full_q, full_k, full_v, full_o, full_up, full_down = (
        lax.all_gather(w_query, "wide", axis=0, tiled=True),
        lax.all_gather(w_key, "wide", axis=0, tiled=True),
        lax.all_gather(w_value, "wide", axis=0, tiled=True),
        lax.all_gather(w_out, "wide", axis=1, tiled=True),
        lax.all_gather(w_up, "wide", axis=0, tiled=True),
        lax.all_gather(w_down, "wide", axis=1, tiled=True),
    )
    grad_y = cotangent.astype(jnp.float32)
    grad_m, gain_m, bias_m = normalize_back(grad_y, unit_m, inv_m, norm_gain[3])
    seq_gm = grads_in(grad_m.astype(jnp.bfloat16))
    grad_act = contract_cols(seq_gm, full_down)
    grad_pre = gelu_back(grad_act)[0].astype(jnp.bfloat16)
    grad_down = contract_rows(active, seq_gm)
    grad_up = contract_rows(seq_c, grad_pre)
    grad_c = input_sum(((grad_pre, full_up),))
    grad_more, gain_c, bias_c = normalize_back(grad_c, unit_c, inv_c, norm_gain[2])
    grad_h = grad_y + grad_more
    grad_z, gain_z, bias_z = normalize_back(grad_h, unit_z, inv_z, norm_gain[1])
    seq_gz = grads_in(grad_z.astype(jnp.bfloat16))
    grad_att = contract_cols(seq_gz, full_o).astype(jnp.bfloat16)
    grad_o = contract_rows(attended, seq_gz)
    grad_queries, grad_keys, grad_values = attend_back(
        queries, key_rows, value_rows, grad_att, totals, block_rows
    )
    grad_q = contract_rows(seq_a, grad_queries)
    grad_k = contract_rows(seq_a, grad_keys)
    grad_v = contract_rows(seq_a, grad_values)
    grad_a = input_sum(((grad_queries, full_q), (grad_keys, full_k), (grad_values, full_v)))
    grad_first, gain_a, bias_a = normalize_back(grad_a, unit_a, inv_a, norm_gain[0])
    input_grad = grad_h + grad_first
    grad_q, grad_k, grad_v, grad_o, grad_up, grad_down = (
        lax.psum_scatter(grad_q, "wide", scatter_dimension=0, tiled=True),
        lax.psum_scatter(grad_k, "wide", scatter_dimension=0, tiled=True),
        lax.psum_scatter(grad_v, "wide", scatter_dimension=0, tiled=True),
        lax.psum_scatter(grad_o, "wide", scatter_dimension=1, tiled=True),
        lax.psum_scatter(grad_up, "wide", scatter_dimension=0, tiled=True),
        lax.psum_scatter(grad_down, "wide", scatter_dimension=1, tiled=True),
    )
    gain_grad, bias_grad = lax.psum(
        (jnp.stack([gain_a, gain_z, gain_c, gain_m]), jnp.stack([bias_a, bias_z, bias_c, bias_m])),
        ("wide", "head"),
    )
    return (
        block_out,
        input_grad,
        grad_q,
        grad_k,
        grad_v,
        grad_o,
        grad_up,
        grad_down,
        gain_grad,
        bias_grad,
    )


def solution(mesh):
    in_specs = (
        P(("wide", "head"), None),
        P(("wide", "head"), None),
        P("wide", "head"),
        P("wide", "head"),
        P("wide", "head"),
        P("head", "wide"),
        P("wide", "head"),
        P("head", "wide"),
        P(),
        P(),
    )
    out_specs = (
        P(("wide", "head"), None),
        P(("wide", "head"), None),
        P("wide", "head"),
        P("wide", "head"),
        P("wide", "head"),
        P("head", "wide"),
        P("wide", "head"),
        P("head", "wide"),
        P(),
        P(),
    )
    return jax.shard_map(
        on_device, mesh=mesh, in_specs=in_specs, out_specs=out_specs, check_vma=False
    )
```

profile of v0, /device:TPU:0, one launch (start us, length us, event | category | flops | bytes accessed | tf_op | source)
XLA Modules:
  0.0 1443.2 jit_solution(8579794204711242059)
XLA Ops:
  15.8 12.4 all_gather.38
  47.9 11.1 all_gather.40
  63.0 36.4 %all-gather.7.cloned.1.call-done = bf16[2048,1024]{1,0:T(8,128)(2,1)} async-done(((bf16[512,1024]{1,0:T(8,128)(2,1)}), bf16[2048,1024]{1,0:T(8,128)(2,1)}) %all-gather.7.cloned.1.call-update) | async-done | bytes 4194320 | tf_op jit(solution)/shard_map/all_gather | solution.py:30
  159.6 142.6 %reduce-scatter.11.cloned.1.call-done = f32[512,1024]{1,0:T(8,128)} async-done(((f32[2048,1024]{1,0:T(8,128)}), f32[512,1024]{1,0:T(8,128)}) %reduce-scatter.11.cloned.1.call-update) | async-done | bytes 2097168 | tf_op jit(solution)/shard_map/reduce_scatter | solution.py:38
  310.9 80.5 %all-gather.9.cloned.1.call-done = bf16[2048,1024]{1,0:T(8,128)(2,1)} async-done(((bf16[512,1024]{1,0:T(8,128)(2,1)}), bf16[2048,1024]{1,0:T(8,128)(2,1)}) %all-gather.9.cloned.1.call-update) | async-done | bytes 4194320 | tf_op jit(solution)/shard_map/all_gather | solution.py:30
  391.4 10.6 fusion.121
  402.0 17.6 %all-gather.13.cloned.1.call-done = bf16[1024,1024]{1,0:T(8,128)(2,1)} async-done(((bf16[1024,128]{1,0:T(8,128)(2,1)}), bf16[1024,1024]{1,0:T(8,128)(2,1)}) %all-gather.13.cloned.1.call-update) | async-done | bytes 2097168 | tf_op jit(solution)/shard_map/all_gather | solution.py:164
  419.6 12.7 fusion.110
  432.4 144.6 %reduce-scatter.13.cloned.1.call-done = f32[512,1024]{1,0:T(8,128)} async-done(((f32[2048,1024]{1,0:T(8,128)}), f32[512,1024]{1,0:T(8,128)}) %reduce-scatter.13.cloned.1.call-update) | async-done | bytes 2097168 | tf_op jit(solution)/shard_map/reduce_scatter | solution.py:38
  586.8 81.0 %all-gather.15.cloned.1.call-done = bf16[2048,1024]{1,0:T(8,128)(2,1)} async-done(((bf16[512,1024]{1,0:T(8,128)(2,1)}), bf16[2048,1024]{1,0:T(8,128)(2,1)}) %all-gather.15.cloned.1.call-update) | async-done | bytes 4194320 | tf_op jit(solution)/shard_map/all_gather | solution.py:34
  667.8 12.6 fusion.10
  689.4 143.1 %reduce-scatter.15.cloned.1.call-done = f32[512,1024]{1,0:T(8,128)} async-done(((f32[2048,1024]{1,0:T(8,128)}), f32[512,1024]{1,0:T(8,128)}) %reduce-scatter.15.cloned.1.call-update) | async-done | bytes 2097168 | tf_op jit(solution)/shard_map/reduce_scatter | solution.py:53
  841.6 81.2 %all-gather.17.cloned.1.call-done = bf16[2048,1024]{1,0:T(8,128)(2,1)} async-done(((bf16[512,1024]{1,0:T(8,128)(2,1)}), bf16[2048,1024]{1,0:T(8,128)(2,1)}) %all-gather.17.cloned.1.call-update) | async-done | bytes 4194320 | tf_op jit(solution)/shard_map/all_gather | solution.py:34
  938.6 11.1 multiply_reduce_fusion.1
  998.0 10.4 multiply_convert_fusion
  1024.3 10.1 fusion.129
  1034.5 12.1 fusion.109
  1066.9 100.1 %reduce-scatter.17.cloned.1.call-done = f32[512,1024]{1,0:T(8,128)} async-done(((f32[2048,1024]{1,0:T(8,128)}), f32[512,1024]{1,0:T(8,128)}) %reduce-scatter.17.cloned.1.call-update) | async-done | bytes 2097168 | tf_op jit(solution)/shard_map/reduce_scatter | solution.py:53
  1169.7 41.8 %all-reduce.2 = (f32[4,1024]{1,0:T(4,128)}, f32[4,1024]{1,0:T(4,128)}) all-reduce(f32[4,1024]{1,0:T(4,128)S(1)} %pad_maximum_fusion.2, f32[4,1024]{1,0:T(4,128)S(1)} %pad_maximum_fusion.3), channel_id=1, replica_groups=mesh['wide'=8,'head'=4] {'wide','head'}, use_global_device_ids=true, to_apply=%region_42.43 | all-reduce | flops 8192 | bytes 65536 | tf_op jit(solution)/shard_map/psum | solution.py:225
  1222.7 54.7 %reduce-scatter.29.cloned.1.call-done = f32[1024,128]{1,0:T(8,128)} async-done(((f32[1024,1024]{1,0:T(8,128)}), f32[1024,128]{1,0:T(8,128)}) %reduce-scatter.29.cloned.1.call-update) | async-done | bytes 524304 | tf_op jit(solution)/shard_map/reduce_scatter | solution.py:223
  1277.5 39.5 %reduce-scatter.25.cloned.1.call-done = f32[256,128]{1,0:T(8,128)} async-done(((f32[256,1024]{1,0:T(8,128)}), f32[256,128]{1,0:T(8,128)}) %reduce-scatter.25.cloned.1.call-update) | async-done | bytes 131088 | tf_op jit(solution)/shard_map/reduce_scatter | solution.py:221
  1317.0 39.7 %reduce-scatter.23.cloned.1.call-done = f32[128,256]{1,0:T(8,128)} async-done(((f32[1024,256]{1,0:T(8,128)}), f32[128,256]{1,0:T(8,128)}) %reduce-scatter.23.cloned.1.call-update) | async-done | bytes 131088 | tf_op jit(solution)/shard_map/reduce_scatter | solution.py:220
  1356.7 39.5 %reduce-scatter.21.cloned.1.call-done = f32[128,256]{1,0:T(8,128)} async-done(((f32[1024,256]{1,0:T(8,128)}), f32[128,256]{1,0:T(8,128)}) %reduce-scatter.21.cloned.1.call-update) | async-done | bytes 131088 | tf_op jit(solution)/shard_map/reduce_scatter | solution.py:219
  1396.2 39.7 %reduce-scatter.19.cloned.1.call-done = f32[128,256]{1,0:T(8,128)} async-done(((f32[1024,256]{1,0:T(8,128)}), f32[128,256]{1,0:T(8,128)}) %reduce-scatter.19.cloned.1.call-update) | async-done | bytes 131088 | tf_op jit(solution)/shard_map/reduce_scatter | solution.py:218
  (315 shorter events, 241.2 us)
Async XLA Ops:
  8.0 91.3 %all-gather.7.cloned.1.call-start = ((), (), s32[]{:S(2)}) async-start(), calls=%async_computation.10 | async-start | bytes 5242880 | tf_op jit(solution)/shard_map/all_gather | solution.py:30
  15.7 286.6 %reduce-scatter.11.cloned.1.call-start = ((), (), s32[]{:S(2)}) async-start(), calls=%async_computation.11 | async-start | bytes 10485760 | tf_op jit(solution)/shard_map/reduce_scatter | solution.py:38
  159.0 147.0 %copy-start.7 = (bf16[512,1024]{1,0:T(8,128)(2,1)S(1)}, bf16[512,1024]{1,0:T(8,128)(2,1)}, u32[]{:S(2)}) copy-start(bf16[512,1024]{1,0:T(8,128)(2,1)} %param.30) | copy-start | bytes 3145732
  159.0 151.9 %all-gather.11.cloned.1.call-start = ((), (), s32[]{:S(2)}) async-start(), calls=%async_computation.13 | async-start | bytes 2359296 | tf_op jit(solution)/shard_map/all_gather | solution.py:163
  159.6 231.8 %all-gather.9.cloned.1.call-start = ((), (), s32[]{:S(2)}) async-start(), calls=%async_computation.12 | async-start | bytes 5242880 | tf_op jit(solution)/shard_map/all_gather | solution.py:30
  310.1 109.6 %all-gather.13.cloned.1.call-start = ((), (), s32[]{:S(2)}) async-start(), calls=%async_computation.14 | async-start | bytes 2359296 | tf_op jit(solution)/shard_map/all_gather | solution.py:164
  310.7 266.4 %reduce-scatter.13.cloned.1.call-start = ((), (), s32[]{:S(2)}) async-start(), calls=%async_computation.15 | async-start | bytes 10485760 | tf_op jit(solution)/shard_map/reduce_scatter | solution.py:38
  432.3 148.6 %copy-start.17 = (bf16[512,1024]{1,0:T(8,128)(2,1)S(1)}, bf16[512,1024]{1,0:T(8,128)(2,1)}, u32[]{:S(2)}) copy-start(bf16[512,1024]{1,0:T(8,128)(2,1)} %param.31) | copy-start | bytes 3145732
  432.4 235.4 %all-gather.15.cloned.1.call-start = ((), (), s32[]{:S(2)}) async-start(), calls=%async_computation.16 | async-start | bytes 5242880 | tf_op jit(solution)/shard_map/all_gather | solution.py:34
  586.3 246.2 %reduce-scatter.15.cloned.1.call-start = ((), (), s32[]{:S(2)}) async-start(), calls=%async_computation.17 | async-start | bytes 10485760 | tf_op jit(solution)/shard_map/reduce_scatter | solution.py:53
  689.4 233.5 %all-gather.17.cloned.1.call-start = ((), (), s32[]{:S(2)}) async-start(), calls=%async_computation.18 | async-start | bytes 5242880 | tf_op jit(solution)/shard_map/all_gather | solution.py:34
  841.5 325.5 %reduce-scatter.17.cloned.1.call-start = ((), (), s32[]{:S(2)}) async-start(), calls=%async_computation.19 | async-start | bytes 10485760 | tf_op jit(solution)/shard_map/reduce_scatter | solution.py:53
  1023.8 198.9 %reduce-scatter.27.cloned.1.call-start = ((), (), s32[]{:S(2)}) async-start(), calls=%async_computation.24 | async-start | bytes 4718592 | tf_op jit(solution)/shard_map/reduce_scatter | solution.py:222
  1034.4 243.1 %reduce-scatter.29.cloned.1.call-start = ((), (), s32[]{:S(2)}) async-start(), calls=%async_computation.25 | async-start | bytes 4718592 | tf_op jit(solution)/shard_map/reduce_scatter | solution.py:223
  1046.6 270.4 %reduce-scatter.25.cloned.1.call-start = ((), (), s32[]{:S(2)}) async-start(), calls=%async_computation.23 | async-start | bytes 1179648 | tf_op jit(solution)/shard_map/reduce_scatter | solution.py:221
  1052.3 304.4 %reduce-scatter.23.cloned.1.call-start = ((), (), s32[]{:S(2)}) async-start(), calls=%async_computation.22 | async-start | bytes 1179648 | tf_op jit(solution)/shard_map/reduce_scatter | solution.py:220
  1057.2 339.1 %reduce-scatter.21.cloned.1.call-start = ((), (), s32[]{:S(2)}) async-start(), calls=%async_computation.21 | async-start | bytes 1179648 | tf_op jit(solution)/shard_map/reduce_scatter | solution.py:219
  1062.0 105.0 %copy-start.8 = (bf16[512,1024]{1,0:T(8,128)(2,1)S(1)}, bf16[512,1024]{1,0:T(8,128)(2,1)}, u32[]{:S(2)}) copy-start(bf16[512,1024]{1,0:T(8,128)(2,1)} %param.30) | copy-start | bytes 3145732
  1062.0 105.0 %copy-start.59 = (f32[1,1024]{1,0:T(1,128)S(1)}, f32[1,1024]{1,0:T(1,128)}, u32[]{:S(2)}) copy-start(f32[1,1024]{1,0:T(1,128)} %copy-done.58) | copy-start | bytes 12292
  1062.1 105.0 %copy-start.65 = (f32[512]{0:T(512)S(1)}, f32[512]{0:T(512)}, u32[]{:S(2)}) copy-start(f32[512]{0:T(512)} %copy-done.64) | copy-start | bytes 6148
  1062.1 105.0 %copy-start.68 = (f32[512]{0:T(512)S(1)}, f32[512]{0:T(512)}, u32[]{:S(2)}) copy-start(f32[512]{0:T(512)} %copy-done.67) | copy-start | bytes 6148
  1062.1 373.9 %reduce-scatter.19.cloned.1.call-start = ((), (), s32[]{:S(2)}) async-start(), calls=%async_computation.20 | async-start | bytes 1179648 | tf_op jit(solution)/shard_map/reduce_scatter | solution.py:218
  1066.8 102.8 %copy-start.71 = (f32[1024]{0:T(1024)S(1)}, f32[1024]{0:T(1024)}, u32[]{:S(2)}) copy-start(f32[1024]{0:T(1024)} %get-tuple-element.135) | copy-start | bytes 12292
  1066.8 144.7 %copy-start.12 = (f32[512,1024]{1,0:T(8,128)S(1)}, f32[512,1024]{1,0:T(8,128)}, u32[]{:S(2)}) copy-start(f32[512,1024]{1,0:T(8,128)} %copy-done.11) | copy-start | bytes 6291460
  (79 other events, 1299.1 us)
Sparse Core Ops, SparseCore 0:
  15.8 83.4 all-gather.6
  159.1 143.0 reduce-scatter.10
  586.4 81.2 all-gather.14
  689.5 143.0 reduce-scatter.14
Sparse Core Ops, SparseCore 1:
  161.4 26.1 all-gather.10
  310.2 81.2 all-gather.8
  393.2 26.4 all-gather.12
  432.4 144.6 reduce-scatter.12
  841.6 81.2 all-gather.16
  1023.9 143.1 reduce-scatter.16
  1170.8 51.9 reduce-scatter.26
  1226.5 50.9 reduce-scatter.28
  1281.1 35.9 reduce-scatter.24
  1320.8 35.9 reduce-scatter.22
  1360.3 35.9 reduce-scatter.20
  1400.0 35.9 reduce-scatter.18
where the time goes:
time: 1450 us; the launch traced here: 1440 us
  waiting for transfers between devices  1050 us (72%)
  matrix products  193 us (13%)
  blocking collectives  85 us (6%)
  other arithmetic  81.8 us (6%)
  between operations  16.8 us (1%)
  local copies, waits for them, and re-layouts  15.2 us (1%)
    reduce_scatter x2, waiting for transfers between devices, branch_sum(): lax.psum_scatter(jnp.dot(left_op, right_op, preferred_element_type=jnp.fl...  287 us
    reduce_scatter x2, waiting for transfers between devices, input_sum(): return lax.psum_scatter(summed, 'head', scatter_dimension=0, tiled=True)  243 us
    all_gather x2, waiting for transfers between devices, grads_in(): return lax.all_gather(values, 'head', axis=0, tiled=True)  162 us
    all_gather x2, waiting for transfers between devices, rows_in(): return lax.all_gather(values, 'head', axis=0, tiled=True)  117 us
    reduce_scatter x1, waiting for transfers between devices, on_device(): lax.psum_scatter(grad_down, 'wide', scatter_dimension=1, tiled=True)  54.7 us
    psum x1, blocking collectives, on_device(): lax.psum((jnp.stack([gain_a, gain_z, gain_c, gain_m]), jnp.stack([bias_a,...  41.8 us
    dot_general x6, matrix products, contract_rows(): lax.dot_general(left_op, right_op, (((0,), (0,)), ((), ())), preferred_el...  40.8 us
    reduce_scatter x1, waiting for transfers between devices, on_device(): lax.psum_scatter(grad_v, 'wide', scatter_dimension=0, tiled=True)  39.7 us
  transfers between devices with their start and end apart: 16, of which 15 were waited for; matrix products, arithmetic and copies ran while one was open for 5% of the time, Pallas kernels for 0%

commit v1 on v0

--- a/solution.py
+++ b/solution.py
@@ -6,6 +6,28 @@
 
 HD = 64
 EPS = 1e-05
+
+
+def laid_out(blocks, dim):
+    shape = list(blocks.shape[1:])
+    shape[dim] *= blocks.shape[0]
+    return jnp.moveaxis(blocks, 0, dim).reshape(shape)
+
+
+def ring_gather(x, axis, dim):
+    size = lax.axis_size(axis)
+    pairs = [(i, (i + 1) % size) for i in range(size)]
+    back = [(b, a) for a, b in pairs]
+    lower, upper = ([], [])
+    for step in range(size - 1):
+        if step % 2 == 0:
+            lower.append(lax.ppermute(lower[-1] if lower else x, axis, pairs))
+        else:
+            upper.append(lax.ppermute(upper[-1] if upper else x, axis, back))
+    blocks = jnp.stack([*lower[::-1], x, *upper])
+    shift = lax.axis_index(axis) - len(lower)
+    blocks = blocks[(jnp.arange(size) - shift) % size]
+    return laid_out(blocks, dim)
 
 
 def normalize(values, gain, bias):
@@ -27,7 +49,7 @@
 
 
 def rows_in(values):
-    return lax.all_gather(values, "head", axis=0, tiled=True)
+    return ring_gather(values, "head", 0)
 
 
 def grads_in(values):

time: 1450 us -> 1430 us (0.986)
  waiting for transfers between devices: 1050 us -> 984 us
  starting transfers between devices: 1.84 us -> 34.1 us
    all_gather x2 -> x0, waiting for transfers between devices: 117 us -> none  [rows_in(): return lax.all_gather(values, 'head', axis=0, tiled=True)]
    ppermute x0 -> x6, waiting for transfers between devices: none -> 69.4 us  [the longest x4 68.8 us: ring_gather(): lower.append(lax.ppermute(lower[-1] if lower else x, axis, pairs))]
    ppermute x0 -> x6, starting transfers between devices: none -> 32.5 us  [the longest x4 24.6 us: ring_gather(): lower.append(lax.ppermute(lower[-1] if lower else x, axis, pairs))]
    all_gather x1, waiting for transfers between devices: 17.6 us -> 0.01 us  [on_device(): lax.all_gather(w_down, 'wide', axis=1, tiled=True)]
  transfers between devices with their start and end apart: 16 -> 20, of which waited for: 15 -> 17; matrix products, arithmetic and copies ran while one was open for 5% -> 5% of each run, Pallas kernels for 0% -> 0%
where the time goes in v1:
time: 1430 us
  waiting for transfers between devices  984 us (69%)
  matrix products  193 us (13%)
  other arithmetic  87.8 us (6%)
  blocking collectives  83.3 us (6%)
  starting transfers between devices  34.1 us (2%)
  local copies, waits for them, and re-layouts  25.9 us (2%)
  between operations  17.2 us (1%)
    reduce_scatter x2, waiting for transfers between devices, branch_sum(): lax.psum_scatter(jnp.dot(left_op, right_op, preferred_element_type=jnp.fl...  285 us
    reduce_scatter x2, waiting for transfers between devices, input_sum(): return lax.psum_scatter(summed, 'head', scatter_dimension=0, tiled=True)  244 us
    all_gather x2, waiting for transfers between devices, grads_in(): return lax.all_gather(values, 'head', axis=0, tiled=True)  162 us
    ppermute x4, waiting for transfers between devices, ring_gather(): lower.append(lax.ppermute(lower[-1] if lower else x, axis, pairs))  68.8 us
    reduce_scatter x1, waiting for transfers between devices, on_device(): lax.psum_scatter(grad_down, 'wide', scatter_dimension=1, tiled=True)  55 us
    psum x1, blocking collectives, on_device(): lax.psum((jnp.stack([gain_a, gain_z, gain_c, gain_m]), jnp.stack([bias_a,...  41.9 us
    dot_general x6, matrix products, contract_rows(): lax.dot_general(left_op, right_op, (((0,), (0,)), ((), ())), preferred_el...  40.5 us
    reduce_scatter x1, waiting for transfers between devices, on_device(): lax.psum_scatter(grad_o, 'wide', scatter_dimension=1, tiled=True)  39.8 us
  transfers between devices with their start and end apart: 20, of which 17 were waited for; matrix products, arithmetic and copies ran while one was open for 5% of the time, Pallas kernels for 0%

profile of v1, /device:TPU:0, one launch (start us, length us, event | category | flops | bytes accessed | tf_op | source)
XLA Modules:
  0.0 1425.2 jit_solution(17862721521302118122)
XLA Ops:
  20.9 10.9 all_gather.31
  51.5 10.8 all_gather.33
  72.1 21.4 %collective-permute-done.1 = bf16[512,1024]{1,0:T(8,128)(2,1)S(1)} collective-permute-done((bf16[512,1024]{1,0:T(8,128)(2,1)}, bf16[512,1024]{1,0:T(8,128)(2,1)S(1)}, u32[]{:S(2)}, u32[]{:S(2)}) %collective-permute-start.1) | collective-permute-done | bytes 1048608 | tf_op jit(solution)/shard_map/ppermute | solution.py:24
  163.5 141.8 %reduce-scatter.11.cloned.1.call-done = f32[512,1024]{1,0:T(8,128)} async-done(((f32[2048,1024]{1,0:T(8,128)}), f32[512,1024]{1,0:T(8,128)}) %reduce-scatter.11.cloned.1.call-update) | async-done | bytes 2097168 | tf_op jit(solution)/shard_map/reduce_scatter | solution.py:60
  316.0 24.0 %collective-permute-done.3 = bf16[512,1024]{1,0:T(8,128)(2,1)S(1)} collective-permute-done((bf16[512,1024]{1,0:T(8,128)(2,1)S(1)}, bf16[512,1024]{1,0:T(8,128)(2,1)S(1)}, u32[]{:S(2)}, u32[]{:S(2)}) %collective-permute-start.3) | collective-permute-done | bytes 1048608 | tf_op jit(solution)/shard_map/ppermute | solution.py:24
  340.0 21.4 %collective-permute-start.4 = (bf16[512,1024]{1,0:T(8,128)(2,1)S(1)}, bf16[512,1024]{1,0:T(8,128)(2,1)S(1)}, u32[]{:S(2)}, u32[]{:S(2)}) collective-permute-start(bf16[512,1024]{1,0:T(8,128)(2,1)S(1)} %collective-permute-done.3), channel_id=1, source_target_pairs={{0,1},{1,2},{2,3},{3,0},{4,5},{5,6},{6,7},{7,4},{8,9},{9,10},{10,1... | collective-permute-start | bytes 3145736 | tf_op jit(solution)/shard_map/ppermute | solution.py:24
  362.4 21.0 %collective-permute-done.4 = bf16[512,1024]{1,0:T(8,128)(2,1)S(1)} collective-permute-done((bf16[512,1024]{1,0:T(8,128)(2,1)S(1)}, bf16[512,1024]{1,0:T(8,128)(2,1)S(1)}, u32[]{:S(2)}, u32[]{:S(2)}) %collective-permute-start.4) | collective-permute-done | bytes 1048608 | tf_op jit(solution)/shard_map/ppermute | solution.py:24
  390.7 10.6 fusion.128
  401.3 12.7 fusion.117
  414.2 143.6 %reduce-scatter.13.cloned.1.call-done = f32[512,1024]{1,0:T(8,128)} async-done(((f32[2048,1024]{1,0:T(8,128)}), f32[512,1024]{1,0:T(8,128)}) %reduce-scatter.13.cloned.1.call-update) | async-done | bytes 2097168 | tf_op jit(solution)/shard_map/reduce_scatter | solution.py:60
  567.2 81.5 %all-gather.9.cloned.1.call-done = bf16[2048,1024]{1,0:T(8,128)(2,1)} async-done(((bf16[512,1024]{1,0:T(8,128)(2,1)}), bf16[2048,1024]{1,0:T(8,128)(2,1)}) %all-gather.9.cloned.1.call-update) | async-done | bytes 4194320 | tf_op jit(solution)/shard_map/all_gather | solution.py:56
  648.6 12.6 fusion.10
  670.3 143.2 %reduce-scatter.15.cloned.1.call-done = f32[512,1024]{1,0:T(8,128)} async-done(((f32[2048,1024]{1,0:T(8,128)}), f32[512,1024]{1,0:T(8,128)}) %reduce-scatter.15.cloned.1.call-update) | async-done | bytes 2097168 | tf_op jit(solution)/shard_map/reduce_scatter | solution.py:75
  823.0 81.0 %all-gather.11.cloned.1.call-done = bf16[2048,1024]{1,0:T(8,128)(2,1)} async-done(((bf16[512,1024]{1,0:T(8,128)(2,1)}), bf16[2048,1024]{1,0:T(8,128)(2,1)}) %all-gather.11.cloned.1.call-update) | async-done | bytes 4194320 | tf_op jit(solution)/shard_map/all_gather | solution.py:56
  919.5 11.1 multiply_reduce_fusion.1
  978.4 10.4 multiply_convert_fusion
  1014.8 12.1 fusion.116
  1047.1 100.5 %reduce-scatter.17.cloned.1.call-done = f32[512,1024]{1,0:T(8,128)} async-done(((f32[2048,1024]{1,0:T(8,128)}), f32[512,1024]{1,0:T(8,128)}) %reduce-scatter.17.cloned.1.call-update) | async-done | bytes 2097168 | tf_op jit(solution)/shard_map/reduce_scatter | solution.py:75
  1150.3 41.9 %all-reduce.2 = (f32[4,1024]{1,0:T(4,128)}, f32[4,1024]{1,0:T(4,128)}) all-reduce(f32[4,1024]{1,0:T(4,128)S(1)} %pad_maximum_fusion.4, f32[4,1024]{1,0:T(4,128)S(1)} %pad_maximum_fusion.5), channel_id=1, replica_groups=mesh['wide'=8,'head'=4] {'wide','head'}, use_global_device_ids=true, to_apply=%region_42.43 | all-reduce | flops 8192 | bytes 65536 | tf_op jit(solution)/shard_map/psum | solution.py:247
  1203.7 55.0 %reduce-scatter.29.cloned.1.call-done = f32[1024,128]{1,0:T(8,128)} async-done(((f32[1024,1024]{1,0:T(8,128)}), f32[1024,128]{1,0:T(8,128)}) %reduce-scatter.29.cloned.1.call-update) | async-done | bytes 524304 | tf_op jit(solution)/shard_map/reduce_scatter | solution.py:245
  1258.8 39.8 %reduce-scatter.25.cloned.1.call-done = f32[256,128]{1,0:T(8,128)} async-done(((f32[256,1024]{1,0:T(8,128)}), f32[256,128]{1,0:T(8,128)}) %reduce-scatter.25.cloned.1.call-update) | async-done | bytes 131088 | tf_op jit(solution)/shard_map/reduce_scatter | solution.py:243
  1298.5 39.6 %reduce-scatter.23.cloned.1.call-done = f32[128,256]{1,0:T(8,128)} async-done(((f32[1024,256]{1,0:T(8,128)}), f32[128,256]{1,0:T(8,128)}) %reduce-scatter.23.cloned.1.call-update) | async-done | bytes 131088 | tf_op jit(solution)/shard_map/reduce_scatter | solution.py:242
  1338.1 39.8 %reduce-scatter.21.cloned.1.call-done = f32[128,256]{1,0:T(8,128)} async-done(((f32[1024,256]{1,0:T(8,128)}), f32[128,256]{1,0:T(8,128)}) %reduce-scatter.21.cloned.1.call-update) | async-done | bytes 131088 | tf_op jit(solution)/shard_map/reduce_scatter | solution.py:241
  1377.9 39.6 %reduce-scatter.19.cloned.1.call-done = f32[128,256]{1,0:T(8,128)} async-done(((f32[1024,256]{1,0:T(8,128)}), f32[128,256]{1,0:T(8,128)}) %reduce-scatter.19.cloned.1.call-update) | async-done | bytes 131088 | tf_op jit(solution)/shard_map/reduce_scatter | solution.py:240
  (339 shorter events, 281.7 us)
Async XLA Ops:
  8.1 297.2 %reduce-scatter.11.cloned.1.call-start = ((), (), s32[]{:S(2)}) async-start(), calls=%async_computation.10 | async-start | bytes 10485760 | tf_op jit(solution)/shard_map/reduce_scatter | solution.py:60
  15.7 56.3 %collective-permute-start.2 = (bf16[512,1024]{1,0:T(8,128)(2,1)}, bf16[512,1024]{1,0:T(8,128)(2,1)}, u32[]{:S(2)}, u32[]{:S(2)}) collective-permute-start(bf16[512,1024]{1,0:T(8,128)(2,1)} %fusion.61), channel_id=1, source_target_pairs={{1,0},{2,1},{3,2},{0,3},{5,4},{6,5},{7,6},{4,7},{9,8},{10,9},{11,1... | collective-permute-start | bytes 3145736 | tf_op jit(solution)/shard_map/ppermute | solution.py:26
  20.8 46.1 %collective-permute-start = (bf16[512,1024]{1,0:T(8,128)(2,1)}, bf16[512,1024]{1,0:T(8,128)(2,1)}, u32[]{:S(2)}, u32[]{:S(2)}) collective-permute-start(bf16[512,1024]{1,0:T(8,128)(2,1)} %fusion.61), channel_id=1, source_target_pairs={{0,1},{1,2},{2,3},{3,0},{4,5},{5,6},{6,7},{7,4},{8,9},{9,10},{10,1... | collective-permute-start | bytes 3145736 | tf_op jit(solution)/shard_map/ppermute | solution.py:24
  66.9 26.6 %collective-permute-start.1 = (bf16[512,1024]{1,0:T(8,128)(2,1)}, bf16[512,1024]{1,0:T(8,128)(2,1)S(1)}, u32[]{:S(2)}, u32[]{:S(2)}) collective-permute-start(bf16[512,1024]{1,0:T(8,128)(2,1)} %collective-permute-done), channel_id=1, source_target_pairs={{0,1},{1,2},{2,3},{3,0},{4,5},{5,6},{6,7},{7,4},{8,9},{9,10},{10,1... | collective-permute-start | bytes 3145736 | tf_op jit(solution)/shard_map/ppermute | solution.py:24
  162.3 228.4 %all-gather.5.cloned.1.call-start = ((), (), s32[]{:S(2)}) async-start(), calls=%async_computation.11 | async-start | bytes 2359296 | tf_op jit(solution)/shard_map/all_gather | solution.py:185
  162.9 238.4 %all-gather.7.cloned.1.call-start = ((), (), s32[]{:S(2)}) async-start(), calls=%async_computation.12 | async-start | bytes 2359296 | tf_op jit(solution)/shard_map/all_gather | solution.py:186
  163.5 394.4 %reduce-scatter.13.cloned.1.call-start = ((), (), s32[]{:S(2)}) async-start(), calls=%async_computation.13 | async-start | bytes 10485760 | tf_op jit(solution)/shard_map/reduce_scatter | solution.py:60
  312.1 27.9 %collective-permute-start.3 = (bf16[512,1024]{1,0:T(8,128)(2,1)S(1)}, bf16[512,1024]{1,0:T(8,128)(2,1)S(1)}, u32[]{:S(2)}, u32[]{:S(2)}) collective-permute-start(bf16[512,1024]{1,0:T(8,128)(2,1)S(1)} %add_convert_fusion.1), channel_id=1, source_target_pairs={{0,1},{1,2},{2,3},{3,0},{4,5},{5,6},{6,7},{7,4},{8,9},{9,10},{10,1... | collective-permute-start | bytes 3145736 | tf_op jit(solution)/shard_map/ppermute | solution.py:24
  313.2 49.2 %collective-permute-start.5 = (bf16[512,1024]{1,0:T(8,128)(2,1)S(1)}, bf16[512,1024]{1,0:T(8,128)(2,1)S(1)}, u32[]{:S(2)}, u32[]{:S(2)}) collective-permute-start(bf16[512,1024]{1,0:T(8,128)(2,1)S(1)} %add_convert_fusion.1), channel_id=1, source_target_pairs={{1,0},{2,1},{3,2},{0,3},{5,4},{6,5},{7,6},{4,7},{9,8},{10,9},{11,1... | collective-permute-start | bytes 3145736 | tf_op jit(solution)/shard_map/ppermute | solution.py:26
  340.0 43.4 %collective-permute-start.4 = (bf16[512,1024]{1,0:T(8,128)(2,1)S(1)}, bf16[512,1024]{1,0:T(8,128)(2,1)S(1)}, u32[]{:S(2)}, u32[]{:S(2)}) collective-permute-start(bf16[512,1024]{1,0:T(8,128)(2,1)S(1)} %collective-permute-done.3), channel_id=1, source_target_pairs={{0,1},{1,2},{2,3},{3,0},{4,5},{5,6},{6,7},{7,4},{8,9},{9,10},{10,1... | collective-permute-start | bytes 3145736 | tf_op jit(solution)/shard_map/ppermute | solution.py:24
  414.0 147.8 %copy-start.17 = (bf16[512,1024]{1,0:T(8,128)(2,1)S(1)}, bf16[512,1024]{1,0:T(8,128)(2,1)}, u32[]{:S(2)}) copy-start(bf16[512,1024]{1,0:T(8,128)(2,1)} %param.31) | copy-start | bytes 3145732
  414.0 234.6 %all-gather.9.cloned.1.call-start = ((), (), s32[]{:S(2)}) async-start(), calls=%async_computation.14 | async-start | bytes 5242880 | tf_op jit(solution)/shard_map/all_gather | solution.py:56
  567.1 246.4 %reduce-scatter.15.cloned.1.call-start = ((), (), s32[]{:S(2)}) async-start(), calls=%async_computation.15 | async-start | bytes 10485760 | tf_op jit(solution)/shard_map/reduce_scatter | solution.py:75
  670.2 233.7 %all-gather.11.cloned.1.call-start = ((), (), s32[]{:S(2)}) async-start(), calls=%async_computation.16 | async-start | bytes 5242880 | tf_op jit(solution)/shard_map/all_gather | solution.py:56
  822.4 325.2 %reduce-scatter.17.cloned.1.call-start = ((), (), s32[]{:S(2)}) async-start(), calls=%async_computation.17 | async-start | bytes 10485760 | tf_op jit(solution)/shard_map/reduce_scatter | solution.py:75
  1004.4 199.4 %reduce-scatter.27.cloned.1.call-start = ((), (), s32[]{:S(2)}) async-start(), calls=%async_computation.22 | async-start | bytes 4718592 | tf_op jit(solution)/shard_map/reduce_scatter | solution.py:244
  1014.7 244.0 %reduce-scatter.29.cloned.1.call-start = ((), (), s32[]{:S(2)}) async-start(), calls=%async_computation.23 | async-start | bytes 4718592 | tf_op jit(solution)/shard_map/reduce_scatter | solution.py:245
  1026.9 271.6 %reduce-scatter.25.cloned.1.call-start = ((), (), s32[]{:S(2)}) async-start(), calls=%async_computation.21 | async-start | bytes 1179648 | tf_op jit(solution)/shard_map/reduce_scatter | solution.py:243
  1032.7 305.4 %reduce-scatter.23.cloned.1.call-start = ((), (), s32[]{:S(2)}) async-start(), calls=%async_computation.20 | async-start | bytes 1179648 | tf_op jit(solution)/shard_map/reduce_scatter | solution.py:242
  1037.4 340.5 %reduce-scatter.21.cloned.1.call-start = ((), (), s32[]{:S(2)}) async-start(), calls=%async_computation.19 | async-start | bytes 1179648 | tf_op jit(solution)/shard_map/reduce_scatter | solution.py:241
  1042.2 375.2 %reduce-scatter.19.cloned.1.call-start = ((), (), s32[]{:S(2)}) async-start(), calls=%async_computation.18 | async-start | bytes 1179648 | tf_op jit(solution)/shard_map/reduce_scatter | solution.py:240
  1042.3 105.3 %copy-start.8 = (bf16[512,1024]{1,0:T(8,128)(2,1)S(1)}, bf16[512,1024]{1,0:T(8,128)(2,1)}, u32[]{:S(2)}) copy-start(bf16[512,1024]{1,0:T(8,128)(2,1)} %param.30) | copy-start | bytes 3145732
  1042.3 105.3 %copy-start.65 = (f32[1,1024]{1,0:T(1,128)S(1)}, f32[1,1024]{1,0:T(1,128)}, u32[]{:S(2)}) copy-start(f32[1,1024]{1,0:T(1,128)} %copy-done.64) | copy-start | bytes 12292
  1047.0 145.2 %copy-start.12 = (f32[512,1024]{1,0:T(8,128)S(1)}, f32[512,1024]{1,0:T(8,128)}, u32[]{:S(2)}) copy-start(f32[512,1024]{1,0:T(8,128)} %copy-done.11) | copy-start | bytes 6291460
  (88 other events, 1795.5 us)
Sparse Core Ops, SparseCore 0:
  162.4 142.8 reduce-scatter.10
  414.1 143.7 reduce-scatter.12
  567.2 81.3 all-gather.8
  670.4 143.0 reduce-scatter.14
  822.6 81.3 all-gather.10
  1004.5 143.0 reduce-scatter.16
  1151.6 52.1 reduce-scatter.26
  1207.7 51.0 reduce-scatter.28
  1262.5 35.9 reduce-scatter.24
  1302.1 35.9 reduce-scatter.22
  1341.9 35.9 reduce-scatter.20
  1381.5 35.9 reduce-scatter.18
Sparse Core Ops, SparseCore 1:
  164.7 25.8 all-gather.4
  192.3 27.9 all-gather.6
